TPU v7x, 256 devices: a whole 4x4x8 slice. The times are simulated.
256 devices in a mesh: dom: 64 (over x_lo, z, y), orb: 4 (over x_hi, core).
Axes of the slice: x: 4 (x_hi: 2, x_lo: 2; x = x_hi * 2 + x_lo), y: 4, z: 8, core: 2. Of those that a mesh axis runs over, the one named last changes fastest.
Arguments:
- orbitals: bfloat16 [128, 4, 1024, 512], P('dom', None, None, 'orb'), may hold values from -6 to 6
- slot_ids: int32 [128, 4], P('dom'), may hold values from 0 to 15, as said below
- slot_count: int32 [128], P('dom'), may hold values from 1 to 4, as said below
- band_tiles: bfloat16 [16, 3, 512, 512], P(None, None, 'dom', 'orb'), may hold values from -0.15625 to 0.15625
- pattern: int32 [16, 3], replicated, may hold values 0 or 1
- occupation: float32 [16, 512], P(None, 'orb'), may hold values from 0.0005 to 0.005
Outputs:
- rotated: bfloat16 [128, 4, 1024, 512], P('dom', None, None, 'orb')
- density: float32 [128, 1024], P('dom')
Inputs may be any that keep to these rules, and one draw needn't show every extreme that they name: `slot_ids`: each row names 4 consecutive orbital blocks counted modulo 16: slot l holds (s + l) mod 16, where the first block s of a grid block may be any of the 16 blocks. The slots in use on grid block g are its first slot_count[g]; some grid block uses all 4.
All inputs are finite; a program needn't handle non-finite values.
Results may differ from a plain program's by a relative error of at most 0.00094.
Values may be sent and summed in bfloat16 or wider, within the bound.
No kernel may reach another device: no remote copies, remote signals or barrier semaphores. Data moves between devices by JAX's collectives and lax.ppermute only.
A program may use at most 128 MiB of HBM per device.

v0:
```python
import jax
import jax.numpy as jnp
from jax import lax
from jax.sharding import Mesh
from jax.sharding import PartitionSpec as P

DOM = ("dom_0", "dom_1", "dom_2")


def laid_out(tiles, dim):
    shape = list(tiles.shape[1:])
    shape[dim] *= tiles.shape[0]
    return jnp.moveaxis(tiles, 0, dim).reshape(shape)


def all_blocks(x, axes, sequence):
    tiles = x
    for k in sequence:
        tiles = lax.all_gather(tiles, axes[k])
    done = sequence[::-1]
    back = [done.index(k) for k in range(len(axes))]
    tiles = tiles.transpose(*back, *range(len(axes), tiles.ndim))
    return tiles.reshape(-1, *x.shape)


def whole_of(x, axes, sequence, dim):
    return laid_out(all_blocks(x, axes, sequence), dim)


def from_everyone(x, axis):
    peers = lax.axis_size(axis)
    return lax.all_to_all(jnp.broadcast_to(x[None], (peers, *x.shape)), axis, 0, 0, tiled=True)


def of_everyone(x, axis):
    return from_everyone(x, axis).sum(axis=0)


def select_tiles(band_full, pattern, slot_ids, slot_count):
    slots_per = slot_ids.shape[1]
    band_count = pattern.shape[1]
    half_band = (band_count - 1) // 2
    active = jnp.arange(slots_per, dtype=jnp.int32)[None, :] < slot_count[:, None]
    source = slot_ids[:, :, None]
    target = slot_ids[:, None, :]
    offset = target - source + half_band
    inside = (offset >= 0) & (offset < band_count)
    column = jnp.clip(offset, 0, band_count - 1)
    keeping = inside & (pattern[source, column] == 1) & active[:, :, None] & active[:, None, :]
    picked = band_full[source, column]
    return jnp.where(keeping[:, :, :, None, None], picked, jnp.zeros((), picked.dtype))


def rotate(values, tile_set):
    return jnp.einsum("glpi,glmij->gmpj", values, tile_set, preferred_element_type=jnp.float32)


def local(orbitals, slot_ids, slot_count, band_tiles, pattern, occupation):
    all_rows = whole_of(band_tiles, DOM, (0, 1, 2), 2)
    tile_set = select_tiles(all_rows, pattern, slot_ids, slot_count)
    rotated_f = rotate(lax.all_gather(orbitals, "orb", axis=3, tiled=True), tile_set)
    rotated = rotated_f.astype(jnp.bfloat16)
    onehot = (
        slot_ids[:, :, None] == jnp.arange(occupation.shape[0], dtype=jnp.int32)[None, None, :]
    ).astype(jnp.float32)
    weights = jnp.einsum("glb,bj->glj", onehot, occupation, precision=lax.Precision.HIGHEST)
    widened = rotated.astype(jnp.float32)
    square = widened * widened
    partial_density = jnp.einsum("gmpj,gmj->gp", square, weights, precision=lax.Precision.HIGHEST)
    density = of_everyone(partial_density, "orb")
    return (rotated, density)


def solution(mesh):
    torus = Mesh(
        mesh.devices.reshape(2, 8, 4, mesh.shape["orb"]), ("dom_0", "dom_1", "dom_2", "orb")
    )
    return jax.shard_map(
        local,
        mesh=torus,
        in_specs=(
            P(DOM, None, None, "orb"),
            P(DOM, None),
            P(DOM),
            P(None, None, DOM, "orb"),
            P(),
            P(None, "orb"),
        ),
        out_specs=(P(DOM, None, None, "orb"), P(DOM, None)),
        check_vma=False,
    )
```

profile of v0, /device:TPU:1, one launch (start us, length us, event | category | flops | bytes accessed | tf_op | source)
XLA Modules:
  0.0 223.0 jit_solution(2459626745871815533)
XLA Ops:
  7.2 0.0 copy-start
  7.2 0.0 copy-start.2
  7.2 0.0 copy-start.1
  7.2 0.0 copy-start.3
  7.2 0.0 all-gather.9.cloned.1.call-start
  7.3 6.5 %all-gather = bf16[32,3,8,128]{3,2,1,0:T(8,128)(2,1)} all-gather(bf16[16,3,8,128]{3,2,1,0:T(8,128)(2,1)} %param.9), channel_id=2, replica_groups=mesh['dom_0'=2,'dom_1'=8,'dom_2'=4,'orb'=4] {'dom_0'}, dimensions={0}, use_global_device_ids=true | all-gather | bytes 294912 | tf_op jit(solution)/shard_map/all_gather | solution.py:19
  13.7 0.0 all-gather.9.cloned.1.call-update
  13.8 0.0 all-gather.11.cloned.1.call-start
  13.8 39.6 %all-gather.9.cloned.1.call-done = bf16[16,16,3,8,128]{4,3,2,1,0:T(8,128)(2,1)} async-done(((bf16[2,16,3,8,128]{4,3,2,1,0:T(8,128)(2,1)}), bf16[16,16,3,8,128]{4,3,2,1,0:T(8,128)(2,1)}) %all-gather.9.cloned.1.call-update) | async-done | bytes 1572880 | tf_op jit(solution)/shard_map/all_gather | solution.py:19
  53.4 0.0 all-gather.11.cloned.1.call-update
  53.4 0.0 all-gather.7.cloned.1.call-start
  53.5 0.7 all-gather.7.cloned.1.call-update
  54.2 0.7 fusion.26
  54.8 0.8 fusion.17
  55.7 0.1 reshape.85
  55.8 0.8 gather_fusion
  56.5 0.1 reshape.101
  56.6 0.1 iota_compare_fusion.2
  56.7 0.1 fusion.23
  56.8 0.2 fusion.13
  57.0 68.7 %all-gather.11.cloned.1.call-done = bf16[32,2,16,3,8,128]{5,4,3,2,1,0:T(8,128)(2,1)} async-done(((bf16[8,2,16,3,8,128]{5,4,3,2,1,0:T(8,128)(2,1)}), bf16[32,2,16,3,8,128]{5,4,3,2,1,0:T(8,128)(2,1)}) %all-gather.11.cloned.1.call-update) | async-done | bytes 6291472 | tf_op jit(solution)/shard_map/all_gather | solution.py:19
  125.7 3.9 %copy.25 = bf16[2,8,4,16,3,8,128]{6,5,4,3,2,1,0:T(8,128)(2,1)S(1)} copy(bf16[2,8,4,16,3,8,128]{6,5,4,3,0,1,2:T(8,128)(2,1)} %bitcast.43) | data formatting | bytes 12582912 | tf_op jit(solution)/shard_map/transpose | solution.py:22
  129.6 4.9 %copy_bitcast_fusion = bf16[16,3,512,128]{3,2,1,0:T(8,128)(2,1)} fusion(bf16[2,8,4,16,3,8,128]{6,5,4,3,2,1,0:T(8,128)(2,1)S(1)} %copy.25), kind=kLoop, calls=%fused_computation.4 | loop fusion | bytes 12582912 | tf_op jit(solution)/shard_map/reshape | solution.py:13
  134.5 5.8 %gather_fusion.1 = bf16[32,512,128]{2,1,0:T(8,128)(2,1)} fusion(bf16[16,3,512,128]{3,2,1,0:T(8,128)(2,1)} %copy_bitcast_fusion, s32[32]{0:T(128)S(1)} %reshape.85), kind=kCustom, calls=%fused_computation.1 | custom fusion | bytes 8388864 | tf_op jit(solution)/shard_map/gather | solution.py:50
  140.3 54.4 %all-gather.7.cloned.1.call-done = bf16[2,4,1024,512]{3,2,1,0:T(8,128)(2,1)} async-done(((bf16[2,4,1024,128]{3,2,1,0:T(8,128)(2,1)}), bf16[2,4,1024,512]{3,2,1,0:T(8,128)(2,1)}) %all-gather.7.cloned.1.call-update) | async-done | bytes 8388624 | tf_op jit(solution)/shard_map/all_gather | solution.py:61
  194.7 9.8 %fusion.7 = bf16[2,4,1024,128]{2,3,1,0:T(8,128)(2,1)S(1)} fusion(bf16[2,4,1024,512]{3,2,1,0:T(8,128)(2,1)} %all-gather.7.cloned.1.call-done, bf16[2,4,4,512,128]{4,3,2,1,0:T(8,128)(2,1)} %bitcast.44, pred[2,4,4]{2,1,0:T(4,128)(4,1)S(1)} %fusion.23), kind=kOutput, calls=%fused_computation.11 | convolution fusion | flops 4298113024 | bytes 14680096 | tf_op jit(solution)/shard_map/glpi,glmij->gmpj/dot_general | solution.py:55
  204.6 2.5 %fusion.2 = f32[2,1,1024,1]{2,1,3,0:T(1,128)S(1)} fusion(f32[2,4,128,1]{2,3,1,0:T(1,128)S(1)} %bitcast.48, bf16[2,4,1024,128]{2,3,1,0:T(8,128)(2,1)S(1)} %fusion.7), kind=kOutput, calls=%fused_computation.6 | convolution fusion | flops 14680064 | bytes 2109440 | tf_op jit(solution)/shard_map/gmpj,gmj->gp/dot_general | solution.py:69
  207.1 0.6 broadcast_in_dim.15
  207.7 3.5 %all-to-all-start = ((f32[4,2,1024]{2,1,0:T(2,128)}), f32[4,2,1024]{2,1,0:T(2,128)S(1)}, u32[]{:S(2)}, u32[]{:S(2)}) async-start(f32[4,2,1024]{2,1,0:T(2,128)} %broadcast_in_dim.15), calls=%async_computation | async-start | bytes 65536 | tf_op jit(solution)/shard_map/all_to_all | solution.py:32
  211.2 2.5 %copy.29 = bf16[2,4,1024,128]{3,2,1,0:T(8,128)(2,1)} copy(bf16[2,4,1024,128]{2,3,1,0:T(8,128)(2,1)S(1)} %fusion.7) | data formatting | bytes 4194304
  213.7 2.1 all-to-all-done
  215.9 0.6 reduce_sum.9
  (6 shorter events, 0.0 us)
Async XLA Ops:
  7.2 49.6 %copy-start = (f32[16,128]{1,0:T(8,128)S(1)}, f32[16,128]{1,0:T(8,128)}, u32[]{:S(2)}) copy-start(f32[16,128]{1,0:T(8,128)} %param.11) | copy-start | bytes 24580
  7.2 49.5 %copy-start.2 = (s32[2,4]{1,0:T(2,128)S(1)}, s32[2,4]{1,0:T(2,128)}, u32[]{:S(2)}) copy-start(s32[2,4]{1,0:T(2,128)} %param.7) | copy-start | bytes 100
  7.2 48.6 %copy-start.1 = (s32[16,3]{0,1:T(4,128)S(1)}, s32[16,3]{0,1:T(4,128)}, u32[]{:S(2)}) copy-start(s32[16,3]{0,1:T(4,128)} %param.10) | copy-start | bytes 580
  7.2 49.4 %copy-start.3 = (s32[2]{0:T(128)S(1)}, s32[2]{0:T(128)}, u32[]{:S(2)}) copy-start(s32[2]{0:T(128)} %param.8) | copy-start | bytes 28
  7.2 46.2 %all-gather.9.cloned.1.call-start = ((), (), s32[]{:S(2)}) async-start(), calls=%async_computation.2 | async-start | bytes 1769472 | tf_op jit(solution)/shard_map/all_gather | solution.py:19
  13.8 111.9 %all-gather.11.cloned.1.call-start = ((), (), s32[]{:S(2)}) async-start(), calls=%async_computation.3 | async-start | bytes 7864320 | tf_op jit(solution)/shard_map/all_gather | solution.py:19
  53.4 141.3 %all-gather.7.cloned.1.call-start = ((), (), s32[]{:S(2)}) async-start(), calls=%async_computation.1 | async-start | bytes 10485760 | tf_op jit(solution)/shard_map/all_gather | solution.py:61
  207.7 8.2 %all-to-all-start = ((f32[4,2,1024]{2,1,0:T(2,128)}), f32[4,2,1024]{2,1,0:T(2,128)S(1)}, u32[]{:S(2)}, u32[]{:S(2)}) async-start(f32[4,2,1024]{2,1,0:T(2,128)} %broadcast_in_dim.15), calls=%async_computation | async-start | bytes 65536 | tf_op jit(solution)/shard_map/all_to_all | solution.py:32
Sparse Core Ops, SparseCore 0:
  13.9 39.4 all-gather.8
  55.2 70.4 all-gather.10
  127.5 67.1 all-gather.6
where the time goes:
time: 223 us
  waiting for transfers between devices  166 us (74%)
  local copies, waits for them, and re-layouts  18.7 us (8%)
  between operations  13.8 us (6%)
  matrix products  12.5 us (6%)
  blocking collectives  6.49 us (3%)
  starting transfers between devices  3.61 us (2%)
  other arithmetic  2.3 us (1%)
    all_gather x2, waiting for transfers between devices, all_blocks(): tiles = lax.all_gather(tiles, axes[k])  108 us
    all_gather x1, waiting for transfers between devices, local(): lax.all_gather(orbitals, 'orb', axis=3, tiled=True)  54.4 us
    dot_general x1, matrix products, rotate(): jnp.einsum('glpi,glmij->gmpj', values, tile_set, preferred_element_type=j...  9.84 us
    all_gather x1, blocking collectives, all_blocks(): tiles = lax.all_gather(tiles, axes[k])  6.49 us
    gather x1, local copies, waits for them, and re-layouts, select_tiles(): picked = band_full[source, column]  5.83 us
    reshape x1, local copies, waits for them, and re-layouts, laid_out(): return jnp.moveaxis(tiles, 0, dim).reshape(shape)  4.87 us
  transfers between devices with their start and end apart: 4, of which 4 were waited for; matrix products, arithmetic and copies ran while one was open for 9% of the time, Pallas kernels for 0%

commit v1 on v0

--- a/solution.py
+++ b/solution.py
@@ -58,7 +58,12 @@
 def local(orbitals, slot_ids, slot_count, band_tiles, pattern, occupation):
     all_rows = whole_of(band_tiles, DOM, (0, 1, 2), 2)
     tile_set = select_tiles(all_rows, pattern, slot_ids, slot_count)
-    rotated_f = rotate(lax.all_gather(orbitals, "orb", axis=3, tiled=True), tile_set)
+    rotated_f = rotate(
+        jnp.concatenate(
+            lax.all_to_all(jnp.stack([orbitals] * lax.axis_size("orb")), "orb", 0, 0), axis=3
+        ),
+        tile_set,
+    )
     rotated = rotated_f.astype(jnp.bfloat16)
     onehot = (
         slot_ids[:, :, None] == jnp.arange(occupation.shape[0], dtype=jnp.int32)[None, None, :]

time: 223 us -> 234 us (1.049)
  local copies, waits for them, and re-layouts: 18.7 us -> 50.7 us
  waiting for transfers between devices: 166 us -> 134 us
  starting transfers between devices: 3.61 us -> 14.5 us
    all_to_all x0 -> x1, waiting for transfers between devices: none -> 92.3 us  [local(): lax.all_to_all(jnp.stack([orbitals] * lax.axis_size('orb')), 'orb', 0, 0)]
    all_gather x2, waiting for transfers between devices: 108 us -> 39.6 us  [all_blocks(): tiles = lax.all_gather(tiles, axes[k])]
    all_gather x1 -> x0, waiting for transfers between devices: 54.4 us -> none  [local(): lax.all_gather(orbitals, 'orb', axis=3, tiled=True)]
    reshape x0 -> x2, local copies, waits for them, and re-layouts: none -> 25.3 us  [local(): jnp.concatenate(lax.all_to_all(jnp.stack([orbitals] * lax.axis_size('orb'...]
    all_to_all x0 -> x1, starting transfers between devices: none -> 10.2 us  [local(): lax.all_to_all(jnp.stack([orbitals] * lax.axis_size('orb')), 'orb', 0, 0)]
    another operation x0 -> x1, local copies, waits for them, and re-layouts: none -> 6.72 us  [local(): jnp.stack([orbitals] * lax.axis_size('orb'))]
  transfers between devices with their start and end apart: 4 -> 4, of which waited for: 4 -> 3; matrix products, arithmetic and copies ran while one was open for 9% -> 15% of each run, Pallas kernels for 0% -> 0%
where the time goes in v1:
time: 234 us; the launch traced here: 233 us
  waiting for transfers between devices  134 us (57%)
  local copies, waits for them, and re-layouts  50.7 us (22%)
  starting transfers between devices  14.5 us (6%)
  between operations  14.1 us (6%)
  matrix products  12.5 us (5%)
  blocking collectives  6.49 us (3%)
    all_to_all x1, waiting for transfers between devices, local(): lax.all_to_all(jnp.stack([orbitals] * lax.axis_size('orb')), 'orb', 0, 0)  92.3 us
    all_gather x2, waiting for transfers between devices, all_blocks(): tiles = lax.all_gather(tiles, axes[k])  39.6 us
    reshape x2, local copies, waits for them, and re-layouts, local(): jnp.concatenate(lax.all_to_all(jnp.stack([orbitals] * lax.axis_size('orb'...  25.3 us
    all_to_all x1, starting transfers between devices, local(): lax.all_to_all(jnp.stack([orbitals] * lax.axis_size('orb')), 'orb', 0, 0)  10.2 us
    dot_general x1, matrix products, rotate(): jnp.einsum('glpi,glmij->gmpj', values, tile_set, preferred_element_type=j...  9.84 us
    another operation x1, local copies, waits for them, and re-layouts, local(): jnp.stack([orbitals] * lax.axis_size('orb'))  6.72 us
    all_gather x1, blocking collectives, all_blocks(): tiles = lax.all_gather(tiles, axes[k])  6.49 us
    gather x1, local copies, waits for them, and re-layouts, select_tiles(): picked = band_full[source, column]  5.83 us
  transfers between devices with their start and end apart: 4, of which 3 were waited for; matrix products, arithmetic and copies ran while one was open for 15% of the time, Pallas kernels for 0%

profile of v1, /device:TPU:1, one launch (start us, length us, event | category | flops | bytes accessed | tf_op | source)
XLA Modules:
  0.0 233.2 jit_solution(2059287385982845049)
XLA Ops:
  7.2 0.0 copy-start
  7.2 0.0 all-gather.6.cloned.1.call-start
  7.2 6.5 %all-gather = bf16[32,3,8,128]{3,2,1,0:T(8,128)(2,1)} all-gather(bf16[16,3,8,128]{3,2,1,0:T(8,128)(2,1)} %param.9), channel_id=2, replica_groups=mesh['dom_0'=2,'dom_1'=8,'dom_2'=4,'orb'=4] {'dom_0'}, dimensions={0}, use_global_device_ids=true | all-gather | bytes 294912 | tf_op jit(solution)/shard_map/all_gather | solution.py:19
  13.7 0.0 all-gather.6.cloned.1.call-update
  13.7 0.0 all-gather.8.cloned.1.call-start
  13.8 39.6 %all-gather.6.cloned.1.call-done = bf16[16,16,3,8,128]{4,3,2,1,0:T(8,128)(2,1)} async-done(((bf16[2,16,3,8,128]{4,3,2,1,0:T(8,128)(2,1)}), bf16[16,16,3,8,128]{4,3,2,1,0:T(8,128)(2,1)}) %all-gather.6.cloned.1.call-update) | async-done | bytes 1572880 | tf_op jit(solution)/shard_map/all_gather | solution.py:19
  53.4 0.0 all-gather.8.cloned.1.call-update
  53.4 6.7 %stack.2 = bf16[4,2,4,1024,128]{4,3,2,1,0:T(8,128)(2,1)} broadcast(bf16[2,4,1024,128]{3,2,1,0:T(8,128)(2,1)} %param.6), dimensions={1,2,3,4} | broadcast | bytes 10485760 | tf_op jit(solution)/shard_map/stack | solution.py:63
  60.1 10.2 %all-to-all-start = ((bf16[4,2,4,1024,128]{4,3,2,1,0:T(8,128)(2,1)}), bf16[4,2,4,1024,128]{4,3,2,1,0:T(8,128)(2,1)}, u32[]{:S(2)}, u32[]{:S(2)}) async-start(bf16[4,2,4,1024,128]{4,3,2,1,0:T(8,128)(2,1)} %stack.2), calls=%async_computation | async-start | bytes 16777216 | tf_op jit(solution)/shard_map/all_to_all | solution.py:63
  70.3 0.0 copy-done.2
  70.3 0.1 fusion.17
  70.4 0.1 reshape.95
  70.5 0.0 copy-done.1
  70.5 0.8 gather_fusion
  71.3 0.1 reshape.111
  71.4 0.0 copy-done.3
  71.4 0.1 iota_compare_fusion.2
  71.4 0.1 fusion.23
  71.5 0.2 fusion.13
  71.7 92.3 %all-to-all-done = bf16[4,2,4,1024,128]{4,3,2,1,0:T(8,128)(2,1)} async-done(((bf16[4,2,4,1024,128]{4,3,2,1,0:T(8,128)(2,1)}), bf16[4,2,4,1024,128]{4,3,2,1,0:T(8,128)(2,1)}, u32[]{:S(2)}, u32[]{:S(2)}) %all-to-all-start) | async-done | bytes 8388640 | tf_op jit(solution)/shard_map/all_to_all | solution.py:63
  164.1 12.2 %copy.29 = bf16[2,4,1024,4,128]{4,3,2,1,0:T(4,128)(2,1)} copy(bf16[2,4,1024,4,128]{4,2,1,0,3:T(8,128)(2,1)} %bitcast.8) | data formatting | bytes 16777216 | tf_op jit(solution)/shard_map/reshape | solution.py:62
  176.2 13.1 %reshape.112 = bf16[2,4,1024,512,1]{3,2,1,0,4:T(8,128)(2,1)} reshape(bf16[2,4,1024,4,128]{4,3,2,1,0:T(4,128)(2,1)} %copy.29) | data formatting | bytes 16777216 | tf_op jit(solution)/shard_map/reshape | solution.py:62
  189.4 3.9 %copy.27 = bf16[2,8,4,16,3,8,128]{6,5,4,3,2,1,0:T(8,128)(2,1)S(1)} copy(bf16[2,8,4,16,3,8,128]{6,5,4,3,0,1,2:T(8,128)(2,1)} %bitcast.42) | data formatting | bytes 12582912 | tf_op jit(solution)/shard_map/transpose | solution.py:22
  193.2 4.9 %copy_bitcast_fusion = bf16[16,3,512,128]{3,2,1,0:T(8,128)(2,1)} fusion(bf16[2,8,4,16,3,8,128]{6,5,4,3,2,1,0:T(8,128)(2,1)S(1)} %copy.27), kind=kLoop, calls=%fused_computation.4 | loop fusion | bytes 12582912 | tf_op jit(solution)/shard_map/reshape | solution.py:13
  198.1 5.8 %gather_fusion.1 = bf16[32,512,128]{2,1,0:T(8,128)(2,1)} fusion(bf16[16,3,512,128]{3,2,1,0:T(8,128)(2,1)} %copy_bitcast_fusion, s32[32]{0:T(128)S(1)} %reshape.95), kind=kCustom, calls=%fused_computation.1 | custom fusion | bytes 8388864 | tf_op jit(solution)/shard_map/gather | solution.py:50
  204.0 9.8 %fusion.7 = bf16[2,4,1024,128]{2,3,1,0:T(8,128)(2,1)S(1)} fusion(bf16[2,4,1024,512,1]{3,2,1,0,4:T(8,128)(2,1)} %reshape.112, bf16[2,4,4,512,128]{4,3,2,1,0:T(8,128)(2,1)} %bitcast.43, pred[2,4,4]{2,1,0:T(4,128)(4,1)S(1)} %fusion.23), kind=kOutput, calls=%fused_computation.11 | convolution fusion | flops 4298113024 | bytes 14680096 | tf_op jit(solution)/shard_map/glpi,glmij->gmpj/dot_general | solution.py:55
  213.8 2.5 %fusion.2 = f32[2,1,1024,1]{2,1,3,0:T(1,128)S(1)} fusion(f32[2,4,128,1]{2,3,1,0:T(1,128)S(1)} %bitcast.47, bf16[2,4,1024,128]{2,3,1,0:T(8,128)(2,1)S(1)} %fusion.7), kind=kOutput, calls=%fused_computation.6 | convolution fusion | flops 14680064 | bytes 2109440 | tf_op jit(solution)/shard_map/gmpj,gmj->gp/dot_general | solution.py:74
  216.3 0.6 broadcast_in_dim.15
  216.9 4.2 %all-to-all-start.1 = ((f32[4,2,1024]{2,1,0:T(2,128)}), f32[4,2,1024]{2,1,0:T(2,128)S(1)}, u32[]{:S(2)}, u32[]{:S(2)}) async-start(f32[4,2,1024]{2,1,0:T(2,128)} %broadcast_in_dim.15), calls=%async_computation.1 | async-start | bytes 65536 | tf_op jit(solution)/shard_map/all_to_all | solution.py:32
  221.1 2.5 %copy.32 = bf16[2,4,1024,128]{3,2,1,0:T(8,128)(2,1)} copy(bf16[2,4,1024,128]{2,3,1,0:T(8,128)(2,1)S(1)} %fusion.7) | data formatting | bytes 4194304
  223.6 2.1 all-to-all-done.1
  225.8 0.6 reduce_sum.9
  (8 shorter events, 0.0 us)
Async XLA Ops:
  7.2 64.4 %copy-start = (f32[16,128]{1,0:T(8,128)S(1)}, f32[16,128]{1,0:T(8,128)}, u32[]{:S(2)}) copy-start(f32[16,128]{1,0:T(8,128)} %param.11) | copy-start | bytes 24580
  7.2 46.2 %all-gather.6.cloned.1.call-start = ((), (), s32[]{:S(2)}) async-start(), calls=%async_computation.2 | async-start | bytes 1769472 | tf_op jit(solution)/shard_map/all_gather | solution.py:19
  13.7 175.6 %all-gather.8.cloned.1.call-start = ((), (), s32[]{:S(2)}) async-start(), calls=%async_computation.3 | async-start | bytes 7864320 | tf_op jit(solution)/shard_map/all_gather | solution.py:19
  60.1 10.2 %copy-start.2 = (s32[2,4]{1,0:T(2,128)S(1)}, s32[2,4]{1,0:T(2,128)}, u32[]{:S(2)}) copy-start(s32[2,4]{1,0:T(2,128)} %param.7) | copy-start | bytes 100
  60.1 10.4 %copy-start.1 = (s32[16,3]{0,1:T(4,128)S(1)}, s32[16,3]{0,1:T(4,128)}, u32[]{:S(2)}) copy-start(s32[16,3]{0,1:T(4,128)} %param.10) | copy-start | bytes 580
  60.1 103.9 %all-to-all-start = ((bf16[4,2,4,1024,128]{4,3,2,1,0:T(8,128)(2,1)}), bf16[4,2,4,1024,128]{4,3,2,1,0:T(8,128)(2,1)}, u32[]{:S(2)}, u32[]{:S(2)}) async-start(bf16[4,2,4,1024,128]{4,3,2,1,0:T(8,128)(2,1)} %stack.2), calls=%async_computation | async-start | bytes 16777216 | tf_op jit(solution)/shard_map/all_to_all | solution.py:63
  70.3 1.0 copy-start.3
  216.9 8.9 %all-to-all-start.1 = ((f32[4,2,1024]{2,1,0:T(2,128)}), f32[4,2,1024]{2,1,0:T(2,128)S(1)}, u32[]{:S(2)}, u32[]{:S(2)}) async-start(f32[4,2,1024]{2,1,0:T(2,128)} %broadcast_in_dim.15), calls=%async_computation.1 | async-start | bytes 65536 | tf_op jit(solution)/shard_map/all_to_all | solution.py:32
Sparse Core Ops, SparseCore 0:
  13.9 39.4 all-gather.5
  55.2 70.4 all-gather.7
